TPU v7x, 512 devices: a whole 4x8x8 slice. The times are simulated.
512 devices in a mesh: dp: 16 (over z, core), fsdp: 32 (over x, y).
Axes of the slice: x: 4, y: 8, z: 8, core: 2. Of those that a mesh axis runs over, the one named last changes fastest.
Arguments:
- passages: bfloat16 [16, 32, 40, 8, 2048], P('dp', 'fsdp'), may hold values from -6 to 6
- counts: int32 [16, 32], P('dp', 'fsdp'), may hold values from 1 to 40, as said below
- helper_table: int32 [16, 32, 2, 32], P('dp', 'fsdp'), may hold values from -1 to 31, as said below
- norm_gain: float32 [2048], replicated, may hold values from 0.1 to 1.9
- projection: bfloat16 [2048, 2048], P('fsdp'), may hold values from -0.125 to 0.125
- queries: bfloat16 [16, 32, 16, 1024], P('dp', 'fsdp'), may hold values from -140 to 140
- cotangent: bfloat16 [16, 32, 24, 8, 2048], P('dp', 'fsdp'), may hold values from -0.0234375 to 0.0234375
Outputs:
- context: bfloat16 [16, 32, 16, 1024], P('dp', 'fsdp')
- gain_gradient: float32 [2048], P('fsdp')
Inputs may be any that keep to these rules, and one draw needn't show every extreme that they name: `counts`: A question with passages beyond the first 8 has 8 plus that many; some question of every group has 40. `helper_table`: entries at e are -1 exactly when 8 + e is not below the question's count; otherwise row 0 names a device of the same group and row 1 a slot from 0 to 15. No two passages of a group share a device and slot; some device of every group has all 16 slots taken; one question sends at most 1 passages to one device, and some question of every group sends exactly that many to some device.
All inputs are finite; a program needn't handle non-finite values.
Results may differ from a plain program's by a relative error of at most 0.0095.
The roundings to bfloat16 on the way count: a program that leaves them out, or rounds other values in their place, can miss the bound.
Values may be sent and summed in bfloat16 or wider, within the bound.
No kernel may reach another device: no remote copies, remote signals or barrier semaphores. Data moves between devices by JAX's collectives and lax.ppermute only.
A program may use at most 64 MiB of HBM per device.

v0:
```python
import jax
import jax.numpy as jnp
from jax import lax
from jax.sharding import Mesh
from jax.sharding import PartitionSpec as P

D = 2048
HEADS = 32
HEAD_DIM = 32
HW = 1024
DEC = 16
LEN = 8
PMAX = 40
KEEP = 8
HELP = 16
ENC = 24
DP = ("dp_0", "dp_1")
EPSILON = 1e-06


def cut_along(array, dim, peers):
    dims = array.shape
    parts = array.reshape(*dims[:dim], peers, dims[dim] // peers, *dims[dim + 1 :])
    return jnp.moveaxis(parts, dim, 0)


def sent_and_summed(array, axis, dim):
    peers = lax.axis_size(axis)
    parts = lax.all_to_all(cut_along(array, dim, peers), axis, 0, 0, tiled=True)
    return jnp.sum(parts, axis=0)


def by_axis(array, axes):
    for axis in axes:
        array = lax.psum(array, axis)
    return array


def normalize(states):
    values = states.astype(jnp.float32)
    scaling = lax.rsqrt(jnp.mean(values * values, axis=-1, keepdims=True) + EPSILON)
    return values * scaling


def rank_slots(helpers, alive_mask, peer_count, per_peer):
    onehot = (
        (helpers[:, None] == lax.iota(jnp.int32, peer_count)[None, :]) & alive_mask[:, None]
    ).astype(jnp.int32)
    before = jnp.cumsum(onehot, axis=0) - onehot
    ranking = jnp.sum(before * onehot, axis=1)
    target = helpers * per_peer + ranking
    places = lax.iota(jnp.int32, peer_count * per_peer)
    return (places[:, None] == target[None, :]) & alive_mask[None, :]


def shards(passages, counts, helper_table, norm_gain, projection, queries, cotangent):
    peer_count = lax.axis_size("fsdp")
    spare_slots = PMAX - KEEP
    per_peer = -(-spare_slots // peer_count)
    stored = passages.reshape(PMAX, LEN, D)
    passage_count = counts.reshape(())
    table_rows = helper_table.reshape(2, spare_slots)
    alive_mask = table_rows[0] >= 0
    selector = rank_slots(table_rows[0], alive_mask, peer_count, per_peer)
    select_matrix = selector.astype(jnp.bfloat16)
    outgoing = jnp.dot(
        select_matrix,
        stored[KEEP:].reshape(spare_slots, LEN * D),
        preferred_element_type=jnp.float32,
    ).astype(jnp.bfloat16)
    slot_tags = jnp.sum(jnp.where(selector, table_rows[1][None, :] + 1, 0), axis=1) - 1
    arrived, arrived_tags = (
        lax.all_to_all(
            outgoing.reshape(peer_count, per_peer, LEN * D),
            "fsdp",
            split_axis=0,
            concat_axis=0,
            tiled=True,
        ),
        lax.all_to_all(
            slot_tags.reshape(peer_count, per_peer), "fsdp", split_axis=0, concat_axis=0, tiled=True
        ),
    )
    pick_matrix = arrived_tags.reshape(-1)[None, :] == lax.iota(jnp.int32, HELP)[:, None]
    helped = jnp.dot(
        pick_matrix.astype(jnp.bfloat16),
        arrived.reshape(-1, LEN * D),
        preferred_element_type=jnp.float32,
    ).astype(jnp.bfloat16)
    encoded = jnp.concatenate([stored[:KEEP], helped.reshape(HELP, LEN, D)], axis=0)
    normal = normalize(encoded).reshape(ENC * LEN, D)
    scaled = (normal * norm_gain).astype(jnp.bfloat16)
    slot_alive = jnp.concatenate(
        [lax.iota(jnp.int32, KEEP) < passage_count, jnp.any(pick_matrix, axis=1)]
    )
    token_alive = jnp.repeat(slot_alive, LEN).astype(jnp.float32)
    upstream = cotangent.reshape(ENC * LEN, 2 * HW)
    weight_piece = lax.all_gather(projection, "fsdp", axis=0, tiled=True)
    partial_states = jnp.dot(scaled, weight_piece, preferred_element_type=jnp.float32)
    back_piece = lax.dot_general(
        upstream, weight_piece, (((1,), (1,)), ((), ())), preferred_element_type=jnp.float32
    )
    row_terms = jnp.dot(token_alive, normal * back_piece, precision=lax.Precision.HIGHEST)
    state_rows = partial_states.astype(jnp.bfloat16).reshape(ENC, LEN * 2 * HW)
    returning = jnp.dot(
        pick_matrix.T.astype(jnp.bfloat16), state_rows[KEEP:], preferred_element_type=jnp.float32
    ).astype(jnp.bfloat16)
    returned = lax.all_to_all(
        returning.reshape(peer_count, per_peer, LEN * 2 * HW),
        "fsdp",
        split_axis=0,
        concat_axis=0,
        tiled=True,
    )
    remote_states = jnp.dot(
        select_matrix.T, returned.reshape(-1, LEN * 2 * HW), preferred_element_type=jnp.float32
    ).astype(jnp.bfloat16)
    all_states = jnp.concatenate([state_rows[:KEEP], remote_states], axis=0).reshape(
        PMAX * LEN, 2, HEADS, HEAD_DIM
    )
    key_rows = all_states[:, 0]
    value_rows = all_states[:, 1]
    query_rows = queries.reshape(DEC, HEADS, HEAD_DIM)
    scores = jnp.einsum(
        "qhd,thd->hqt", query_rows, key_rows, preferred_element_type=jnp.float32
    ) * HEAD_DIM ** (-0.5)
    token_live = jnp.repeat(lax.iota(jnp.int32, PMAX) < passage_count, LEN)
    scores = jnp.where(token_live[None, None, :], scores, -jnp.inf)
    highest = jnp.max(scores, axis=-1, keepdims=True)
    raised = jnp.exp(scores - highest)
    weights = (raised / jnp.sum(raised, axis=-1, keepdims=True)).astype(jnp.bfloat16)
    context = jnp.einsum("hqt,thd->qhd", weights, value_rows, preferred_element_type=jnp.float32)
    context_out = context.astype(jnp.bfloat16).reshape(1, 1, DEC, HW)
    group_share = sent_and_summed(row_terms, "fsdp", 0)
    gradient = by_axis(group_share, DP)
    return (context_out, gradient)


def solution(mesh):
    split = Mesh(mesh.devices.reshape(8, 2, mesh.shape["fsdp"]), ("dp_0", "dp_1", "fsdp"))
    return jax.shard_map(
        shards,
        mesh=split,
        in_specs=(
            P(DP, "fsdp", None, None, None),
            P(DP, "fsdp"),
            P(DP, "fsdp", None, None),
            P(),
            P("fsdp", None),
            P(DP, "fsdp", None, None),
            P(DP, "fsdp", None, None, None),
        ),
        out_specs=(P(DP, "fsdp", None, None), P("fsdp")),
        check_vma=False,
    )
```

profile of v0, /device:TPU:8, one launch (start us, length us, event | category | flops | bytes accessed | tf_op | source)
XLA Modules:
  0.0 233.3 jit_solution(2594520575006294680)
XLA Ops:
  7.2 0.0 copy-start
  7.2 0.0 all-gather.2.cloned.1.call-start
  7.2 0.7 all-gather.2.cloned.1.call-update
  7.9 0.7 broadcast_compare_fusion
  8.6 0.8 add_bitcast_fusion.1
  9.4 0.1 fusion.29
  9.4 0.1 reduce_window_sum.11
  9.5 0.2 select_reduce_fusion.1
  9.7 0.7 fusion.39
  10.4 0.1 select_reduce_fusion
  10.5 0.7 copy.33
  11.2 10.2 %all-to-all-start = ((s32[32,1,1]{2,1,0:T(1,128)}), s32[32,1,1]{2,1,0:T(1,128)S(1)}, u32[]{:S(2)}, u32[]{:S(2)}) async-start(s32[32,1,1]{2,1,0:T(1,128)} %copy.33), calls=%async_computation | async-start | bytes 32768 | tf_op jit(solution)/shard_map/all_to_all | solution.py:80
  21.4 0.6 copy.46
  22.0 0.4 fusion.1
  22.4 0.5 broadcast.61
  22.9 1.4 reduce.2
  24.4 1.6 reshape.139
  26.0 4.0 %all-to-all-done = s32[32,1,1]{2,1,0:T(1,128)S(1)} async-done(((s32[32,1,1]{2,1,0:T(1,128)}), s32[32,1,1]{2,1,0:T(1,128)S(1)}, u32[]{:S(2)}, u32[]{:S(2)}) %all-to-all-start) | async-done | bytes 160 | tf_op jit(solution)/shard_map/all_to_all | solution.py:80
  29.9 5.9 %all-to-all-start.1 = ((bf16[32,2,8192]{2,1,0:T(2,128)(2,1)}), bf16[32,2,8192]{2,1,0:T(2,128)(2,1)}, u32[]{:S(2)}, u32[]{:S(2)}) async-start(bf16[32,2,8192]{2,1,0:T(2,128)(2,1)} %reshape.139), calls=%async_computation.1 | async-start | bytes 2097152 | tf_op jit(solution)/shard_map/all_to_all | solution.py:73
  36.5 0.7 reduce.1
  37.2 0.1 fusion.30
  37.3 0.1 pad_add_fusion
  37.4 0.1 broadcast_in_dim.45
  37.5 0.1 reshape.135
  37.6 33.8 %all-to-all-done.1 = bf16[32,2,8192]{2,1,0:T(2,128)(2,1)} async-done(((bf16[32,2,8192]{2,1,0:T(2,128)(2,1)}), bf16[32,2,8192]{2,1,0:T(2,128)(2,1)}, u32[]{:S(2)}, u32[]{:S(2)}) %all-to-all-start.1) | async-done | bytes 1048608 | tf_op jit(solution)/shard_map/all_to_all | solution.py:73
  71.4 4.3 %reshape.140 = bf16[32,1,16384]{2,1,0:T(2,128)(2,1)S(1)} reshape(bf16[32,2,8192]{2,1,0:T(2,128)(2,1)} %all-to-all-done.1) | data formatting | bytes 2097152
  75.7 1.2 convolution_convert_fusion.3
  77.0 0.3 copy.47
  77.3 0.2 fusion.7
  77.5 0.1 rsqrt.12
  77.6 51.0 %all-gather.2.cloned.1.call-done = bf16[2048,2048]{1,0:T(8,128)(2,1)} async-done(((bf16[64,2048]{1,0:T(8,128)(2,1)}), bf16[2048,2048]{1,0:T(8,128)(2,1)}) %all-gather.2.cloned.1.call-update) | async-done | bytes 8388624 | tf_op jit(solution)/shard_map/all_gather | solution.py:98
  128.6 5.2 %convolution_convert_fusion.4 = bf16[192,2048]{1,0:T(8,128)(2,1)S(1)} fusion(bf16[2048,2048]{1,0:T(8,128)(2,1)} %all-gather.2.cloned.1.call-done, f32[2048]{0:T(1024)S(1)} %copy-done.12, f32[192]{0:T(256)S(1)} %rsqrt.12, bf16[16,8,2048]{2,1,0:T(8,128)(2,1)S(1)} %bitcast.75, bf16[8,8,2048]{2,1,0:T(8,128)(2,1)S(1)} %slice_bitcast_fusion), kind=kOutput, calls=%fused_computation.9 | convolution fusion | flops 1612972032 | bytes 9970432 | tf_op jit(solution)/shard_map/dot_general | solution.py:99
  133.9 0.2 slice.45
  134.2 0.6 copy-done.5
  134.8 0.2 copy-done.4
  135.0 7.4 %fusion.3 = f32[2048,192]{0,1:T(8,128)} fusion(bf16[2048,2048]{1,0:T(8,128)(2,1)} %all-gather.2.cloned.1.call-done, bf16[1,1,24,8,2048]{4,3,2,1,0:T(8,128)(2,1)S(1)} %copy-done, f32[192]{0:T(256)S(1)} %rsqrt.12, bf16[16,8,2048]{2,1,0:T(8,128)(2,1)S(1)} %bitcast.76, bf16[8,8,2048]{2,1,0:T(8,128)(2,1)S(1)} %copy-done.4), kind=kOutput, calls=%fused_computation.8 | convolution fusion | flops 1612185600 | bytes 11535104 | tf_op jit(solution)/shard_map/dot_general | solution.py:100
  142.4 1.8 copy.40
  144.3 2.0 convolution_bitcast_fusion
  146.3 7.4 %all-to-all-start.3 = ((f32[32,1,64]{2,1,0:T(1,128)}), f32[32,1,64]{2,1,0:T(1,128)S(1)}, u32[]{:S(2)}, u32[]{:S(2)}) async-start(f32[32,1,64]{2,1,0:T(1,128)} %convolution_bitcast_fusion), calls=%async_computation.3 | async-start | bytes 32768 | tf_op jit(solution)/shard_map/all_to_all | solution.py:29
  153.7 0.5 fusion.2
  154.1 1.4 reduce.3
  155.6 1.6 reshape.141
  157.2 5.0 %all-to-all-done.3 = f32[32,1,64]{2,1,0:T(1,128)S(1)} async-done(((f32[32,1,64]{2,1,0:T(1,128)}), f32[32,1,64]{2,1,0:T(1,128)S(1)}, u32[]{:S(2)}, u32[]{:S(2)}) %all-to-all-start.3) | async-done | bytes 8224 | tf_op jit(solution)/shard_map/all_to_all | solution.py:29
  162.2 5.7 %all-to-all-start.2 = ((bf16[32,2,8192]{2,1,0:T(2,128)(2,1)}), bf16[32,2,8192]{2,1,0:T(2,128)(2,1)}, u32[]{:S(2)}, u32[]{:S(2)}) async-start(bf16[32,2,8192]{2,1,0:T(2,128)(2,1)} %reshape.141), calls=%async_computation.2 | async-start | bytes 2097152 | tf_op jit(solution)/shard_map/all_to_all | solution.py:108
  167.9 0.1 broadcast_in_dim.41
  168.0 0.6 broadcast_in_dim.42
  168.6 0.1 reshape.130
  168.8 0.1 slice.43
  168.9 0.1 reduce_sum.49
  169.0 18.1 %psum.14 = f32[64]{0:T(128)S(1)} all-reduce(f32[64]{0:T(128)S(1)} %reduce_sum.49), channel_id=1, replica_groups=mesh['dp_0'=8,'dp_1'=2,'fsdp'=32] {'dp_0'}, use_global_device_ids=true, to_apply=%region_8.9 | all-reduce | flops 64 | bytes 512 | tf_op jit(solution)/shard_map/psum | solution.py:35
  187.1 3.0 %psum.15 = f32[64]{0:T(128)} all-reduce(f32[64]{0:T(128)S(1)} %psum.14), channel_id=1, replica_groups=mesh['dp_0'=8,'dp_1'=2,'fsdp'=32] {'dp_1'}, use_global_device_ids=true, to_apply=%region_9.10 | all-reduce | flops 64 | bytes 512 | tf_op jit(solution)/shard_map/psum | solution.py:35
  190.1 4.8 %all-to-all-done.2 = bf16[32,2,8192]{2,1,0:T(2,128)(2,1)} async-done(((bf16[32,2,8192]{2,1,0:T(2,128)(2,1)}), bf16[32,2,8192]{2,1,0:T(2,128)(2,1)}, u32[]{:S(2)}, u32[]{:S(2)}) %all-to-all-start.2) | async-done | bytes 1048608 | tf_op jit(solution)/shard_map/all_to_all | solution.py:108
  194.9 4.3 %reshape.142 = bf16[32,1,16384]{2,1,0:T(2,128)(2,1)S(1)} reshape(bf16[32,2,8192]{2,1,0:T(2,128)(2,1)} %all-to-all-done.2) | data formatting | bytes 2097152
  199.2 1.4 convolution_convert_fusion
  200.7 0.1 pad_maximum_fusion
  200.8 5.4 %reshape.128 = bf16[320,2,32,32]{3,2,1,0:T(8,128)(2,1)} reshape(bf16[40,16384]{1,0:T(8,128)(2,1)S(1)} %pad_maximum_fusion) | data formatting | bytes 2621440 | tf_op jit(solution)/shard_map/reshape | solution.py:118
  206.2 5.0 %fusion.40 = (bf16[320,1,32,32]{3,2,1,0:T(8,128)(2,1)}, bf16[320,1,32,32]{3,2,1,0:T(8,128)(2,1)S(1)}) fusion(bf16[320,2,32,32]{3,2,1,0:T(8,128)(2,1)} %reshape.128), kind=kLoop, calls=%fused_computation.65 | loop fusion | bytes 2621440 | tf_op jit(solution)/shard_map/slice | solution.py:121
  211.2 5.1 %copy.45 = bf16[320,1,32,32]{0,3,2,1:T(8,128)(2,1)} copy(bf16[320,1,32,32]{3,2,1,0:T(8,128)(2,1)} %get-tuple-element.2) | data formatting | bytes 1310720
  216.2 1.4 fusion.11
  217.6 0.9 copy-done.2
  218.5 0.3 fusion.41
  218.8 4.3 %copy.44 = bf16[320,1,32,32]{0,3,2,1:T(8,128)(2,1)} copy(bf16[320,1,32,32]{3,2,1,0:T(8,128)(2,1)S(1)} %get-tuple-element.3) | data formatting | bytes 1310720
  223.1 2.6 %fusion.12 = bf16[16,32,32]{2,0,1:T(8,128)(2,1)S(1)} fusion(bf16[320,1,32,32]{0,3,2,1:T(8,128)(2,1)} %copy.44, f32[32,16]{1,0:T(8,128)S(1)} %fusion.41, f32[32,16,320]{2,1,0:T(8,128)} %copy-done.2), kind=kOutput, calls=%fused_computation.23 | convolution fusion | flops 10994495 | bytes 1345536 | tf_op jit(solution)/shard_map/hqt,thd->qhd/dot_general | solution.py:132
  225.7 0.8 reshape.131
  (33 shorter events, 0.2 us)
Async XLA Ops:
  7.2 127.6 %copy-start = (bf16[1,1,24,8,2048]{4,3,2,1,0:T(8,128)(2,1)S(1)}, bf16[1,1,24,8,2048]{4,3,2,1,0:T(8,128)(2,1)}, u32[]{:S(2)}) copy-start(bf16[1,1,24,8,2048]{4,3,2,1,0:T(8,128)(2,1)} %param.13) | copy-start | bytes 2359300
  7.2 14.2 %slice-start = ((bf16[1,1,40,8,2048]{4,3,2,1,0:T(8,128)(2,1)}), bf16[1,1,32,8,2048]{4,3,2,1,0:T(8,128)(2,1)S(1)}, s32[]{:S(2)}) async-start(bf16[1,1,40,8,2048]{4,3,2,1,0:T(8,128)(2,1)} %param.7), calls=%async_computation.5 | async-start | bytes 2097152 | tf_op jit(solution)/shard_map/slice | solution.py:68
  7.2 121.4 %all-gather.2.cloned.1.call-start = ((), (), s32[]{:S(2)}) async-start(), calls=%async_computation.4 | async-start | bytes 8650752 | tf_op jit(solution)/shard_map/all_gather | solution.py:98
  8.6 13.4 %copy-start.7 = (pred[32]{0:T(512)(128)(4,1)}, pred[32]{0:T(512)(128)(4,1)S(1)}, u32[]{:S(2)}) copy-start(pred[32]{0:T(512)(128)(4,1)S(1)} %broadcast_compare_fusion) | copy-start | bytes 100
  10.4 11.6 %copy-start.9 = (s32[32]{0:T(128)}, s32[32]{0:T(128)S(1)}, u32[]{:S(2)}) copy-start(s32[32]{0:T(128)S(1)} %fusion.39) | copy-start | bytes 388
  11.2 18.7 %all-to-all-start = ((s32[32,1,1]{2,1,0:T(1,128)}), s32[32,1,1]{2,1,0:T(1,128)S(1)}, u32[]{:S(2)}, u32[]{:S(2)}) async-start(s32[32,1,1]{2,1,0:T(1,128)} %copy.33), calls=%async_computation | async-start | bytes 32768 | tf_op jit(solution)/shard_map/all_to_all | solution.py:80
  24.4 12.1 %copy-start.1 = (bf16[1,1,40,8,2048]{4,3,2,1,0:T(8,128)(2,1)S(1)}, bf16[1,1,40,8,2048]{4,3,2,1,0:T(8,128)(2,1)}, u32[]{:S(2)}) copy-start(bf16[1,1,40,8,2048]{4,3,2,1,0:T(8,128)(2,1)} %param.7) | copy-start | bytes 3932164
  29.9 41.5 %all-to-all-start.1 = ((bf16[32,2,8192]{2,1,0:T(2,128)(2,1)}), bf16[32,2,8192]{2,1,0:T(2,128)(2,1)}, u32[]{:S(2)}, u32[]{:S(2)}) async-start(bf16[32,2,8192]{2,1,0:T(2,128)(2,1)} %reshape.139), calls=%async_computation.1 | async-start | bytes 2097152 | tf_op jit(solution)/shard_map/all_to_all | solution.py:73
  36.5 92.1 %copy-start.3 = (bf16[8,8,2048]{2,1,0:T(8,128)(2,1)}, bf16[8,8,2048]{2,1,0:T(8,128)(2,1)S(1)}, u32[]{:S(2)}) copy-start(bf16[8,8,2048]{2,1,0:T(8,128)(2,1)S(1)} %slice_bitcast_fusion) | copy-start | bytes 786436
  75.7 52.9 %copy-start.12 = (f32[2048]{0:T(1024)S(1)}, f32[2048]{0:T(1024)}, u32[]{:S(2)}) copy-start(f32[2048]{0:T(1024)} %param.10) | copy-start | bytes 24580
  133.8 0.9 copy-start.5
  133.9 1.1 copy-start.4
  146.3 16.0 %all-to-all-start.3 = ((f32[32,1,64]{2,1,0:T(1,128)}), f32[32,1,64]{2,1,0:T(1,128)S(1)}, u32[]{:S(2)}, u32[]{:S(2)}) async-start(f32[32,1,64]{2,1,0:T(1,128)} %convolution_bitcast_fusion), calls=%async_computation.3 | async-start | bytes 32768 | tf_op jit(solution)/shard_map/all_to_all | solution.py:29
  155.6 13.0 %copy-start.6 = (bf16[1,1,16,1024]{3,2,1,0:T(8,128)(2,1)S(1)}, bf16[1,1,16,1024]{3,2,1,0:T(8,128)(2,1)}, u32[]{:S(2)}) copy-start(bf16[1,1,16,1024]{3,2,1,0:T(8,128)(2,1)} %param.12) | copy-start | bytes 98308
  155.6 13.2 %slice-start.1 = ((bf16[192,2048]{1,0:T(8,128)(2,1)}), bf16[64,2048]{1,0:T(8,128)(2,1)S(1)}, s32[]{:S(2)}) async-start(bf16[192,2048]{1,0:T(8,128)(2,1)} %copy-done.5), calls=%async_computation.6 | async-start | bytes 524288 | tf_op jit(solution)/shard_map/slice | solution.py:118
  162.2 32.7 %all-to-all-start.2 = ((bf16[32,2,8192]{2,1,0:T(2,128)(2,1)}), bf16[32,2,8192]{2,1,0:T(2,128)(2,1)}, u32[]{:S(2)}, u32[]{:S(2)}) async-start(bf16[32,2,8192]{2,1,0:T(2,128)(2,1)} %reshape.141), calls=%async_computation.2 | async-start | bytes 2097152 | tf_op jit(solution)/shard_map/all_to_all | solution.py:108
  168.8 30.4 %copy-start.8 = (pred[32]{0:T(512)(128)(4,1)S(1)}, pred[32]{0:T(512)(128)(4,1)}, u32[]{:S(2)}) copy-start(pred[32]{0:T(512)(128)(4,1)} %copy-done.7) | copy-start | bytes 100
  168.8 30.4 %copy-start.10 = (s32[32]{0:T(128)S(1)}, s32[32]{0:T(128)}, u32[]{:S(2)}) copy-start(s32[32]{0:T(128)} %copy-done.9) | copy-start | bytes 388
  211.2 5.1 %copy-start.11 = (pred[320]{0:T(512)(128)(4,1)S(1)}, pred[320]{0:T(512)(128)(4,1)}, u32[]{:S(2)}) copy-start(pred[320]{0:T(512)(128)(4,1)} %broadcast_in_dim.42) | copy-start | bytes 964
  217.6 0.9 copy-start.2
Sparse Core Ops, SparseCore 0:
  11.2 117.3 all-gather.1
where the time goes:
time: 234 us; the launch traced here: 233 us
  waiting for transfers between devices  99.4 us (42%)
  local copies, waits for them, and re-layouts  39.6 us (17%)
  starting transfers between devices  29.1 us (12%)
  matrix products  22.2 us (9%)
  blocking collectives  21.1 us (9%)
  between operations  15 us (6%)
  other arithmetic  6.97 us (3%)
    all_gather x1, waiting for transfers between devices, shards(): weight_piece = lax.all_gather(projection, 'fsdp', axis=0, tiled=True)  51 us
    all_to_all x1, waiting for transfers between devices, shards(): lax.all_to_all(outgoing.reshape(peer_count, per_peer, LEN * D), 'fsdp', s...  33.8 us
    unnamed x34, local copies, waits for them, and re-layouts  23.8 us
    psum x2, blocking collectives, by_axis(): array = lax.psum(array, axis)  21.1 us
    all_to_all x1, starting transfers between devices, shards(): lax.all_to_all(slot_tags.reshape(peer_count, per_peer), 'fsdp', split_axi...  10.2 us
    dot_general x1, matrix products, shards(): lax.dot_general(upstream, weight_piece, (((1,), (1,)), ((), ())), preferr...  7.42 us
    all_to_all x1, starting transfers between devices, sent_and_summed(): parts = lax.all_to_all(cut_along(array, dim, peers), axis, 0, 0, tiled=True)  7.39 us
    all_to_all x1, starting transfers between devices, shards(): lax.all_to_all(outgoing.reshape(peer_count, per_peer, LEN * D), 'fsdp', s...  5.87 us
  transfers between devices with their start and end apart: 5, of which 5 were waited for; matrix products, arithmetic and copies ran while one was open for 8% of the time, Pallas kernels for 0%

commit v1 on v0

--- a/solution.py
+++ b/solution.py
@@ -95,7 +95,14 @@
     )
     token_alive = jnp.repeat(slot_alive, LEN).astype(jnp.float32)
     upstream = cotangent.reshape(ENC * LEN, 2 * HW)
-    weight_piece = lax.all_gather(projection, "fsdp", axis=0, tiled=True)
+    degree = lax.axis_size("fsdp")
+    weight_piece = lax.all_to_all(
+        jnp.tile(projection, tuple((degree if at == 0 else 1 for at in range(projection.ndim)))),
+        "fsdp",
+        tiled=True,
+        split_axis=0,
+        concat_axis=0,
+    )
     partial_states = jnp.dot(scaled, weight_piece, preferred_element_type=jnp.float32)
     back_piece = lax.dot_general(
         upstream, weight_piece, (((1,), (1,)), ((), ())), preferred_element_type=jnp.float32

time: 234 us -> 354 us (1.51)
  the two profiles are of different devices: /device:TPU:8 before, /device:TPU:1 now
where the time goes in v1:
time: 354 us
  waiting for transfers between devices  185 us (52%)
  blocking collectives  57.3 us (16%)
  local copies, waits for them, and re-layouts  43.1 us (12%)
  starting transfers between devices  36.9 us (10%)
  matrix products  22.3 us (6%)
  other arithmetic  7.1 us (2%)
    all_to_all x1, waiting for transfers between devices, shards(): lax.all_to_all(jnp.tile(projection, tuple((degree if at == 0 else 1 for a...  175 us
    all_to_all x1, blocking collectives, shards(): lax.all_to_all(outgoing.reshape(peer_count, per_peer, LEN * D), 'fsdp', s...  29.6 us
    psum x2, blocking collectives, by_axis(): array = lax.psum(array, axis)  27.7 us
    unnamed x36, local copies, waits for them, and re-layouts  23 us
    all_to_all x1, starting transfers between devices, sent_and_summed(): parts = lax.all_to_all(cut_along(array, dim, peers), axis, 0, 0, tiled=True)  13.5 us
    all_to_all x1, starting transfers between devices, shards(): lax.all_to_all(slot_tags.reshape(peer_count, per_peer), 'fsdp', split_axi...  10.5 us
    all_to_all x1, starting transfers between devices, shards(): lax.all_to_all(jnp.tile(projection, tuple((degree if at == 0 else 1 for a...  8.29 us
    dot_general x1, matrix products, shards(): lax.dot_general(upstream, weight_piece, (((1,), (1,)), ((), ())), preferr...  7.52 us
  transfers between devices with their start and end apart: 4, of which 3 were waited for; matrix products, arithmetic and copies ran while one was open for 4% of the time, Pallas kernels for 0%

profile of v1, /device:TPU:1, one launch (start us, length us, event | category | flops | bytes accessed | tf_op | source)
XLA Modules:
  0.0 353.5 jit_solution(9800931553585825884)
XLA Ops:
  0.6 0.0 copy-start
  0.6 0.0 slice-start
  0.7 0.8 broadcast_compare_fusion
  1.5 0.8 add_bitcast_fusion.1
  2.2 0.1 fusion.30
  2.3 0.1 reduce_window_sum.11
  2.4 0.2 select_reduce_fusion.1
  2.5 0.7 fusion.40
  3.2 0.1 select_reduce_fusion
  3.4 0.7 copy.33
  4.1 10.5 %all-to-all-start = ((s32[32,1,1]{2,1,0:T(1,128)}), s32[32,1,1]{2,1,0:T(1,128)S(1)}, u32[]{:S(2)}, u32[]{:S(2)}) async-start(s32[32,1,1]{2,1,0:T(1,128)} %copy.33), calls=%async_computation | async-start | bytes 32768 | tf_op jit(solution)/shard_map/all_to_all | solution.py:80
  14.6 0.6 copy.46
  15.2 0.4 fusion.1
  15.6 0.5 broadcast.102
  16.1 1.4 reduce.2
  17.6 0.0 copy-start.6
  17.6 0.8 reshape.193
  18.4 4.8 %all-to-all-done = s32[32,1,1]{2,1,0:T(1,128)S(1)} async-done(((s32[32,1,1]{2,1,0:T(1,128)}), s32[32,1,1]{2,1,0:T(1,128)S(1)}, u32[]{:S(2)}, u32[]{:S(2)}) %all-to-all-start) | async-done | bytes 160 | tf_op jit(solution)/shard_map/all_to_all | solution.py:80
  23.2 29.6 %all_to_all.34 = bf16[32,2,8192]{2,1,0:T(2,128)(2,1)} all-to-all(bf16[32,2,8192]{2,1,0:T(2,128)(2,1)S(1)} %reshape.193), channel_id=1, replica_groups=mesh['dp_0'=8,'dp_1'=2,'fsdp'=32] {'fsdp'}, dimensions={0} | all-to-all | bytes 2097152 | tf_op jit(solution)/shard_map/all_to_all | solution.py:73
  52.7 4.3 %tile.2 = bf16[32,64,2048]{2,1,0:T(8,128)(2,1)} broadcast(bf16[64,2048]{1,0:T(8,128)(2,1)S(1)} %copy-done.6), dimensions={1,2} | broadcast | bytes 8650752 | tf_op jit(solution)/shard_map/tile | solution.py:100
  57.0 8.3 %all-to-all-start.2 = ((bf16[32,64,2048]{2,1,0:T(8,128)(2,1)}), bf16[32,64,2048]{2,1,0:T(8,128)(2,1)}, u32[]{:S(2)}, u32[]{:S(2)}) async-start(bf16[32,64,2048]{2,1,0:T(8,128)(2,1)} %tile.2), calls=%async_computation.2 | async-start | bytes 16777216 | tf_op jit(solution)/shard_map/all_to_all | solution.py:99
  66.0 0.7 reduce.1
  66.7 0.1 fusion.31
  66.8 0.1 pad_add_fusion
  66.9 0.1 broadcast_in_dim.45
  66.9 0.1 reshape.189
  67.0 4.3 %reshape.194 = bf16[32,1,16384]{2,1,0:T(2,128)(2,1)S(1)} reshape(bf16[32,2,8192]{2,1,0:T(2,128)(2,1)} %all_to_all.34) | data formatting | bytes 2097152
  71.4 1.2 convolution_convert_fusion.3
  72.6 0.3 copy.47
  72.9 0.2 fusion.4
  73.1 0.1 rsqrt.13
  73.2 175.4 %all-to-all-done.2 = bf16[32,64,2048]{2,1,0:T(8,128)(2,1)} async-done(((bf16[32,64,2048]{2,1,0:T(8,128)(2,1)}), bf16[32,64,2048]{2,1,0:T(8,128)(2,1)}, u32[]{:S(2)}, u32[]{:S(2)}) %all-to-all-start.2) | async-done | bytes 8388640 | tf_op jit(solution)/shard_map/all_to_all | solution.py:99
  248.6 5.2 %convolution_convert_fusion.4 = bf16[192,2048]{1,0:T(8,128)(2,1)S(1)} fusion(bf16[2048,2048]{1,0:T(8,128)(2,1)} %bitcast.6, f32[2048]{0:T(1024)S(1)} %copy-done.13, f32[24,8]{1,0:T(8,128)S(1)} %add_rsqrt_fusion, bf16[16,8,2048]{2,1,0:T(8,128)(2,1)S(1)} %bitcast.74, bf16[8,8,2048]{2,1,0:T(8,128)(2,1)S(1)} %slice_bitcast_fusion), kind=kOutput, calls=%fused_computation.9 | convolution fusion | flops 1612972032 | bytes 9970432 | tf_op jit(solution)/shard_map/dot_general | solution.py:106
  253.9 0.2 slice.45
  254.2 0.6 copy-done.5
  254.8 0.3 copy-done.4
  255.0 7.5 %fusion.3 = f32[2048,192]{0,1:T(8,128)} fusion(bf16[2048,2048]{1,0:T(8,128)(2,1)} %bitcast.6, bf16[1,1,24,8,2048]{4,3,2,1,0:T(8,128)(2,1)S(1)} %copy-done, f32[192]{0:T(256)S(1)} %rsqrt.13, bf16[16,8,2048]{2,1,0:T(8,128)(2,1)S(1)} %bitcast.75, bf16[8,8,2048]{2,1,0:T(8,128)(2,1)S(1)} %copy-done.4), kind=kOutput, calls=%fused_computation.8 | convolution fusion | flops 1612185600 | bytes 11535104 | tf_op jit(solution)/shard_map/dot_general | solution.py:107
  262.5 1.8 copy.40
  264.4 2.0 convolution_bitcast_fusion
  266.4 13.5 %all-to-all-start.4 = ((f32[32,1,64]{2,1,0:T(1,128)}), f32[32,1,64]{2,1,0:T(1,128)S(1)}, u32[]{:S(2)}, u32[]{:S(2)}) async-start(f32[32,1,64]{2,1,0:T(1,128)} %convolution_bitcast_fusion), calls=%async_computation.4 | async-start | bytes 32768 | tf_op jit(solution)/shard_map/all_to_all | solution.py:29
  279.9 0.5 fusion.2
  280.3 1.4 reduce.3
  281.8 1.6 reshape.195
  283.4 5.0 %all-to-all-done.4 = f32[32,1,64]{2,1,0:T(1,128)S(1)} async-done(((f32[32,1,64]{2,1,0:T(1,128)}), f32[32,1,64]{2,1,0:T(1,128)S(1)}, u32[]{:S(2)}, u32[]{:S(2)}) %all-to-all-start.4) | async-done | bytes 8224 | tf_op jit(solution)/shard_map/all_to_all | solution.py:29
  288.5 4.7 %all-to-all-start.3 = ((bf16[32,2,8192]{2,1,0:T(2,128)(2,1)}), bf16[32,2,8192]{2,1,0:T(2,128)(2,1)}, u32[]{:S(2)}, u32[]{:S(2)}) async-start(bf16[32,2,8192]{2,1,0:T(2,128)(2,1)} %reshape.195), calls=%async_computation.3 | async-start | bytes 2097152 | tf_op jit(solution)/shard_map/all_to_all | solution.py:115
  293.1 0.1 broadcast_in_dim.41
  293.2 0.6 broadcast_in_dim.42
  293.8 0.1 reshape.184
  294.0 0.1 slice.43
  294.1 0.1 reduce_sum.49
  294.2 21.0 %psum.14 = f32[64]{0:T(128)S(1)} all-reduce(f32[64]{0:T(128)S(1)} %reduce_sum.49), channel_id=1, replica_groups=mesh['dp_0'=8,'dp_1'=2,'fsdp'=32] {'dp_0'}, use_global_device_ids=true, to_apply=%region_8.9 | all-reduce | flops 64 | bytes 512 | tf_op jit(solution)/shard_map/psum | solution.py:35
  315.2 6.7 %psum.15 = f32[64]{0:T(128)} all-reduce(f32[64]{0:T(128)S(1)} %psum.14), channel_id=1, replica_groups=mesh['dp_0'=8,'dp_1'=2,'fsdp'=32] {'dp_1'}, use_global_device_ids=true, to_apply=%region_9.10 | all-reduce | flops 64 | bytes 512 | tf_op jit(solution)/shard_map/psum | solution.py:35
  321.9 4.3 %reshape.196 = bf16[32,1,16384]{2,1,0:T(2,128)(2,1)S(1)} reshape(bf16[32,2,8192]{2,1,0:T(2,128)(2,1)} %all-to-all-done.3) | data formatting | bytes 2097152
  326.2 1.4 convolution_convert_fusion
  327.7 0.1 pad_maximum_fusion
  327.8 5.4 %reshape.182 = bf16[320,2,32,32]{3,2,1,0:T(8,128)(2,1)} reshape(bf16[40,16384]{1,0:T(8,128)(2,1)S(1)} %pad_maximum_fusion) | data formatting | bytes 2621440 | tf_op jit(solution)/shard_map/reshape | solution.py:125
  333.2 5.0 %fusion.41 = (bf16[320,1,32,32]{3,2,1,0:T(8,128)(2,1)}, bf16[320,1,32,32]{3,2,1,0:T(8,128)(2,1)S(1)}) fusion(bf16[320,2,32,32]{3,2,1,0:T(8,128)(2,1)} %reshape.182), kind=kLoop, calls=%fused_computation.67 | loop fusion | bytes 2621440 | tf_op jit(solution)/shard_map/slice | solution.py:128
  338.2 5.1 %copy.45 = bf16[320,1,32,32]{0,3,2,1:T(8,128)(2,1)} copy(bf16[320,1,32,32]{3,2,1,0:T(8,128)(2,1)} %get-tuple-element.2) | data formatting | bytes 1310720
  343.2 1.4 fusion.11
  344.7 0.9 copy-done.2
  345.6 0.3 fusion.42
  345.8 4.3 %copy.44 = bf16[320,1,32,32]{0,3,2,1:T(8,128)(2,1)} copy(bf16[320,1,32,32]{3,2,1,0:T(8,128)(2,1)S(1)} %get-tuple-element.3) | data formatting | bytes 1310720
  350.1 2.6 fusion.12
  352.7 0.8 reshape.185
  (34 shorter events, 0.2 us)
Async XLA Ops:
  0.6 254.1 %copy-start = (bf16[1,1,24,8,2048]{4,3,2,1,0:T(8,128)(2,1)S(1)}, bf16[1,1,24,8,2048]{4,3,2,1,0:T(8,128)(2,1)}, u32[]{:S(2)}) copy-start(bf16[1,1,24,8,2048]{4,3,2,1,0:T(8,128)(2,1)} %param.13) | copy-start | bytes 2359300
  0.6 13.9 %slice-start = ((bf16[1,1,40,8,2048]{4,3,2,1,0:T(8,128)(2,1)}), bf16[1,1,32,8,2048]{4,3,2,1,0:T(8,128)(2,1)S(1)}, s32[]{:S(2)}) async-start(bf16[1,1,40,8,2048]{4,3,2,1,0:T(8,128)(2,1)} %param.7), calls=%async_computation.5 | async-start | bytes 2097152 | tf_op jit(solution)/shard_map/slice | solution.py:68
  1.5 13.7 %copy-start.8 = (pred[32]{0:T(512)(128)(4,1)}, pred[32]{0:T(512)(128)(4,1)S(1)}, u32[]{:S(2)}) copy-start(pred[32]{0:T(512)(128)(4,1)S(1)} %broadcast_compare_fusion) | copy-start | bytes 100
  3.2 11.9 %copy-start.10 = (s32[32]{0:T(128)}, s32[32]{0:T(128)S(1)}, u32[]{:S(2)}) copy-start(s32[32]{0:T(128)S(1)} %fusion.40) | copy-start | bytes 388
  4.1 19.1 %all-to-all-start = ((s32[32,1,1]{2,1,0:T(1,128)}), s32[32,1,1]{2,1,0:T(1,128)S(1)}, u32[]{:S(2)}, u32[]{:S(2)}) async-start(s32[32,1,1]{2,1,0:T(1,128)} %copy.33), calls=%async_computation | async-start | bytes 32768 | tf_op jit(solution)/shard_map/all_to_all | solution.py:80
  17.6 35.1 %copy-start.6 = (bf16[64,2048]{1,0:T(8,128)(2,1)S(1)}, bf16[64,2048]{1,0:T(8,128)(2,1)}, u32[]{:S(2)}) copy-start(bf16[64,2048]{1,0:T(8,128)(2,1)} %param.11) | copy-start | bytes 786436
  57.0 9.0 %copy-start.1 = (bf16[1,1,40,8,2048]{4,3,2,1,0:T(8,128)(2,1)S(1)}, bf16[1,1,40,8,2048]{4,3,2,1,0:T(8,128)(2,1)}, u32[]{:S(2)}) copy-start(bf16[1,1,40,8,2048]{4,3,2,1,0:T(8,128)(2,1)} %param.7) | copy-start | bytes 3932164
  57.0 191.6 %all-to-all-start.2 = ((bf16[32,64,2048]{2,1,0:T(8,128)(2,1)}), bf16[32,64,2048]{2,1,0:T(8,128)(2,1)}, u32[]{:S(2)}, u32[]{:S(2)}) async-start(bf16[32,64,2048]{2,1,0:T(8,128)(2,1)} %tile.2), calls=%async_computation.2 | async-start | bytes 16777216 | tf_op jit(solution)/shard_map/all_to_all | solution.py:99
  66.0 182.6 %copy-start.3 = (bf16[8,8,2048]{2,1,0:T(8,128)(2,1)}, bf16[8,8,2048]{2,1,0:T(8,128)(2,1)S(1)}, u32[]{:S(2)}) copy-start(bf16[8,8,2048]{2,1,0:T(8,128)(2,1)S(1)} %slice_bitcast_fusion) | copy-start | bytes 786436
  71.4 177.3 %copy-start.13 = (f32[2048]{0:T(1024)S(1)}, f32[2048]{0:T(1024)}, u32[]{:S(2)}) copy-start(f32[2048]{0:T(1024)} %param.10) | copy-start | bytes 24580
  253.9 0.9 copy-start.5
  253.9 1.1 copy-start.4
  266.4 22.1 %all-to-all-start.4 = ((f32[32,1,64]{2,1,0:T(1,128)}), f32[32,1,64]{2,1,0:T(1,128)S(1)}, u32[]{:S(2)}, u32[]{:S(2)}) async-start(f32[32,1,64]{2,1,0:T(1,128)} %convolution_bitcast_fusion), calls=%async_computation.4 | async-start | bytes 32768 | tf_op jit(solution)/shard_map/all_to_all | solution.py:29
  281.8 12.0 %copy-start.7 = (bf16[1,1,16,1024]{3,2,1,0:T(8,128)(2,1)S(1)}, bf16[1,1,16,1024]{3,2,1,0:T(8,128)(2,1)}, u32[]{:S(2)}) copy-start(bf16[1,1,16,1024]{3,2,1,0:T(8,128)(2,1)} %param.12) | copy-start | bytes 98308
  281.8 12.2 %slice-start.1 = ((bf16[192,2048]{1,0:T(8,128)(2,1)}), bf16[64,2048]{1,0:T(8,128)(2,1)S(1)}, s32[]{:S(2)}) async-start(bf16[192,2048]{1,0:T(8,128)(2,1)} %copy-done.5), calls=%async_computation.6 | async-start | bytes 524288 | tf_op jit(solution)/shard_map/slice | solution.py:125
  288.5 33.5 %all-to-all-start.3 = ((bf16[32,2,8192]{2,1,0:T(2,128)(2,1)}), bf16[32,2,8192]{2,1,0:T(2,128)(2,1)}, u32[]{:S(2)}, u32[]{:S(2)}) async-start(bf16[32,2,8192]{2,1,0:T(2,128)(2,1)} %reshape.195), calls=%async_computation.3 | async-start | bytes 2097152 | tf_op jit(solution)/shard_map/all_to_all | solution.py:115
  294.0 32.2 %copy-start.9 = (pred[32]{0:T(512)(128)(4,1)S(1)}, pred[32]{0:T(512)(128)(4,1)}, u32[]{:S(2)}) copy-start(pred[32]{0:T(512)(128)(4,1)} %copy-done.8) | copy-start | bytes 100
  294.0 32.2 %copy-start.11 = (s32[32]{0:T(128)S(1)}, s32[32]{0:T(128)}, u32[]{:S(2)}) copy-start(s32[32]{0:T(128)} %copy-done.10) | copy-start | bytes 388
  338.2 5.1 %copy-start.12 = (pred[320]{0:T(512)(128)(4,1)S(1)}, pred[320]{0:T(512)(128)(4,1)}, u32[]{:S(2)}) copy-start(pred[320]{0:T(512)(128)(4,1)} %broadcast_in_dim.42) | copy-start | bytes 964
  344.6 0.9 copy-start.2
